TPU v7x, 32 devices: a whole 2x2x4 slice. The times are simulated.
32 devices in a mesh: member: 2 (over y), lon: 4 (over z), lat: 4 (over x, core).
Axes of the slice: x: 2, y: 2, z: 4, core: 2. Of those that a mesh axis runs over, the one named last changes fastest.
Arguments:
- tracer: float32 [64, 64, 512], P('member', 'lat', 'lon'), parts along dimension 0, may hold values from -6 to 6
- velocity: float32 [2, 64, 64, 512], P(None, 'member', 'lat', 'lon'), parts along dimension 1, may hold values from -0.9 to 0.9
- surface: float32 [128, 512], P(('member', 'lat'), 'lon'), parts along dimension 0, may hold values from -6 to 6
- transport: float32 [4, 64, 512], P('member', 'lat', 'lon'), parts along dimension 0, may hold values from -3 to 3
- horiz_mixing: float32 [64], P('member'), parts along dimension 0, may hold values from 0.03 to 0.2
- vert_mixing: float32 [62], P('member'), parts along dimension 0, may hold values from 0.3 to 30
- levels: int32 [64, 512], P('lat', 'lon'), may hold values from 0 to 32, as said below
- land_tiles: int32 [4, 4], P('lat', 'lon'), may hold values 0 or 1
- fold_pair: int32 [512], P('lon'), may hold values from 0 to 511, as said below
Outputs:
- tracer_new: float32 [64, 64, 512], P('member', 'lat', 'lon'), parts along dimension 0
- surface_new: float32 [128, 512], P(('member', 'lat'), 'lon'), parts along dimension 0
- transport_new: float32 [4, 64, 512], P('member', 'lat', 'lon'), parts along dimension 0
There are 2 independent parts, one for each index of `member`. A program takes and returns all parts, laid end to end along the dimension named above; an argument that names none is the same for every part. Nothing has to cross between parts.
Inputs may be any that keep to these rules, and one draw needn't show every extreme that they name: 0 marks a land cell, otherwise the count of sea levels. The fold pairing is a reflection: fold_pair[i] = (p - i) mod 512 for one p in 0..4095, so fold_pair[fold_pair[i]] = i.
All inputs are finite; a program needn't handle non-finite values. No bound on the sum of `land_tiles` on one device may be relied on, other than what follows from the above.
Results may differ from a plain program's by a relative error of at most 0.00002.
Values sent between devices are 32-bit elements; how exact they have to be, the bound alone decides.
A program may use at most 64 MiB of HBM per device.

v0:
```python
import jax
import jax.numpy as jnp
from jax import lax
from jax.sharding import PartitionSpec as P

SUB = 12


fb_step = 0.6
drag_rate = 0.02


def with_halo(cells, sides, width):
    for axis, dim in sides:
        count = lax.axis_size(axis)
        head = lax.slice_in_dim(cells, 0, width, axis=dim)
        tail = lax.slice_in_dim(cells, cells.shape[dim] - width, cells.shape[dim], axis=dim)
        cells = jnp.concatenate(
            [
                lax.ppermute(tail, axis, [(i, (i + 1) % count) for i in range(count)]),
                cells,
                lax.ppermute(head, axis, [((i + 1) % count, i) for i in range(count)]),
            ],
            axis=dim,
        )
    return cells


def fix_rims(extended, fold_row, at_top, at_bottom):
    south_rim = jnp.where(at_bottom, jnp.zeros_like(extended[..., :1, :]), extended[..., :1, :])
    inner_rim = jnp.where(at_top, fold_row, extended[..., -1:, 1:-1])
    north_rim = jnp.concatenate(
        [extended[..., -1:, :1], inner_rim, extended[..., -1:, -1:]], axis=-1
    )
    return jnp.concatenate([south_rim, extended[..., 1:-1, :], north_rim], axis=-2)


def face_flux(near_side, far_side, wet_near, wet_far, vel_near, vel_far, mixing):
    return (
        wet_near
        * wet_far
        * (mixing * (far_side - near_side) - 0.25 * (vel_near + vel_far) * (near_side + far_side))
    )


def thomas(stepped, coupling):
    depth_count = stepped.shape[0]
    primes = []
    sweeps = []
    for depth_idx in range(depth_count):
        diagonal_term = jnp.ones_like(stepped[depth_idx])
        if depth_idx > 0:
            diagonal_term = diagonal_term + coupling[depth_idx - 1]
        if depth_idx < depth_count - 1:
            diagonal_term = diagonal_term + coupling[depth_idx]
        if depth_idx > 0:
            pivot_term = diagonal_term + coupling[depth_idx - 1] * primes[depth_idx - 1]
            reduced = (
                stepped[depth_idx] + coupling[depth_idx - 1] * sweeps[depth_idx - 1]
            ) / pivot_term
        else:
            pivot_term = diagonal_term
            reduced = stepped[depth_idx] / pivot_term
        if depth_idx < depth_count - 1:
            primes.append(-coupling[depth_idx] / pivot_term)
        else:
            primes.append(jnp.zeros_like(reduced))
        sweeps.append(reduced)
    solved = [None] * depth_count
    solved[depth_count - 1] = sweeps[depth_count - 1]
    for depth_idx in range(depth_count - 2, -1, -1):
        solved[depth_idx] = sweeps[depth_idx] - primes[depth_idx] * solved[depth_idx + 1]
    return jnp.stack(solved)


def many_cycles(height, zonal, merid, level_real, depth_count, north_edge_of):

    def east_side(field):
        return jnp.roll(field, -1, axis=1)

    def west_side(field):
        return jnp.roll(field, 1, axis=1)

    def north_side(field):
        return jnp.concatenate([field[1:], north_edge_of(field[-1:])], axis=0)

    def south_side(field):
        return jnp.concatenate([jnp.zeros_like(field[:1]), field[:-1]], axis=0)

    sea_cells = (level_real > 0).astype(jnp.float32)
    zonal_mask = sea_cells * east_side(sea_cells)
    zonal_depth = (level_real + east_side(level_real)) / (2.0 * depth_count)
    merid_mask = sea_cells * north_side(sea_cells)
    merid_depth = (level_real + north_side(level_real)) / (2.0 * depth_count)

    def one_cycle(substep, state):
        height_now, zonal_now, merid_now = state
        divergence = zonal_now - west_side(zonal_now) + (merid_now - south_side(merid_now))
        height_next = (height_now - fb_step * divergence) * sea_cells
        zonal_next = (
            zonal_now * (1.0 - drag_rate)
            - fb_step * zonal_depth * (east_side(height_next) - height_next)
        ) * zonal_mask
        merid_next = (
            merid_now * (1.0 - drag_rate)
            - fb_step * merid_depth * (north_side(height_next) - height_next)
        ) * merid_mask
        return (height_next, zonal_next, merid_next)

    return lax.fori_loop(0, SUB, one_cycle, (height, zonal, merid))


def shards(
    tracer, velocity, surface, transport, horiz_mixing, vert_mixing, levels, land_tiles, fold_pair
):
    depth_count = tracer.shape[0]
    tile_rows = surface.shape[0]
    tile_cols = surface.shape[1]
    at_top = lax.axis_index("lat") == lax.axis_size("lat") - 1
    at_bottom = lax.axis_index("lat") == 0
    land_flag = land_tiles[0, 0]
    depth_levels = levels * (1 - land_flag)
    level_ext = with_halo(depth_levels, (("lon", 1), ("lat", 0)), 1)
    level_top = lax.all_gather(depth_levels[-1:, :], "lon", axis=1, tiled=True)
    level_pair = jnp.take(level_top, fold_pair, axis=1)
    level_full = fix_rims(level_ext, level_pair, at_top, at_bottom)
    stacked = jnp.concatenate([tracer[None], velocity], axis=0)
    tracer_ext = with_halo(stacked, (("lon", 3), ("lat", 2)), 1)
    top_slab = stacked[:, :, -1:, :]
    tracer_top = lax.all_gather(top_slab, "lon", axis=3, tiled=True)
    tracer_pair = jnp.take(tracer_top, fold_pair, axis=3)
    tracer_full = fix_rims(tracer_ext, tracer_pair, at_top, at_bottom)
    wet_full = (jnp.arange(depth_count, dtype=jnp.int32)[:, None, None] < level_full[None]).astype(
        jnp.float32
    )
    field = tracer_full[0]
    zonal_vel = tracer_full[1]
    merid_vel = tracer_full[2]
    mixing = horiz_mixing[:, None, None]
    flux_east = face_flux(
        field[:, 1:-1, :-1],
        field[:, 1:-1, 1:],
        wet_full[:, 1:-1, :-1],
        wet_full[:, 1:-1, 1:],
        zonal_vel[:, 1:-1, :-1],
        zonal_vel[:, 1:-1, 1:],
        mixing,
    )
    flux_north = face_flux(
        field[:, :-1, 1:-1],
        field[:, 1:, 1:-1],
        wet_full[:, :-1, 1:-1],
        wet_full[:, 1:, 1:-1],
        merid_vel[:, :-1, 1:-1],
        merid_vel[:, 1:, 1:-1],
        mixing,
    )
    wet_here = wet_full[:, 1:-1, 1:-1]
    stepped = wet_here * (
        field[:, 1:-1, 1:-1]
        + (flux_east[:, :, 1:] - flux_east[:, :, :-1] + (flux_north[:, 1:] - flux_north[:, :-1]))
    )
    coupling = vert_mixing[:, None, None] * wet_here[1:]
    tracer_new = thomas(stepped, coupling)
    level_float = depth_levels.astype(jnp.float32)
    deep_ext = with_halo(
        jnp.stack([surface, transport[0], transport[1], level_float]), (("lon", 2), ("lat", 1)), SUB
    )
    row_index = jnp.arange(deep_ext.shape[1], dtype=jnp.int32)[None, :, None]
    deep_ext = jnp.where(at_bottom & (row_index < SUB), 0.0, deep_ext)
    strip_piece = deep_ext[:, : SUB + tile_rows, SUB : SUB + tile_cols]
    pair_row = jnp.broadcast_to(fold_pair.astype(jnp.float32)[None, None, :], (4, 1, tile_cols))
    strip_all = lax.all_gather(
        jnp.concatenate([strip_piece, pair_row], axis=1), "lon", axis=2, tiled=True
    )
    pair_all = strip_all[0, -1].astype(jnp.int32)
    strip_fields = strip_all[:, :-1]
    col_start = lax.axis_index("lon") * tile_cols

    def strip_path():
        results = many_cycles(
            strip_fields[0],
            strip_fields[1],
            strip_fields[2],
            strip_fields[3],
            depth_count,
            lambda edge_row: jnp.take(edge_row, pair_all, axis=1),
        )
        return tuple(
            (
                lax.dynamic_slice(part_field, (SUB, col_start), (tile_rows, tile_cols))
                for part_field in results
            )
        )

    def tile_path():
        results = many_cycles(
            deep_ext[0],
            deep_ext[1],
            deep_ext[2],
            deep_ext[3],
            depth_count,
            lambda edge_row: jnp.zeros_like(edge_row),
        )
        return tuple(
            (part_field[SUB : SUB + tile_rows, SUB : SUB + tile_cols] for part_field in results)
        )

    height, zonal, merid = lax.cond(at_top, strip_path, tile_path)
    return (tracer_new, height, jnp.stack([zonal, merid]))


def solution(mesh):
    return jax.shard_map(
        shards,
        mesh=mesh,
        in_specs=(
            P("member", "lat", "lon"),
            P(None, "member", "lat", "lon"),
            P(("member", "lat"), "lon"),
            P("member", "lat", "lon"),
            P("member"),
            P("member"),
            P("lat", "lon"),
            P("lat", "lon"),
            P("lon"),
        ),
        out_specs=(
            P("member", "lat", "lon"),
            P(("member", "lat"), "lon"),
            P("member", "lat", "lon"),
        ),
        check_vma=False,
    )
```

profile of v0, /device:TPU:7, one launch (start us, length us, event | category | flops | bytes accessed | tf_op | source)
XLA Modules:
  0.0 136.3 jit_solution(15120960949177525387)
XLA Ops:
  0.7 1.7 %fusion.20 = (f32[3,32,16,1]{3,2,1,0:T(8,128)S(1)}, f32[3,32,16,1]{3,2,1,0:T(8,128)S(1)}) fusion(f32[2,32,16,128]{3,2,1,0:T(8,128)} %param.18, f32[1,32,16,128]{3,2,1,0:T(8,128)} %bitcast.97), kind=kLoop, calls=%fused_computation.74 | loop fusion | flops 3072 | bytes 798720 | tf_op jit(solution)/shard_map/concatenate | solution.py:127
  2.4 0.4 copy.95
  2.8 1.3 collective-permute-start.4
  4.2 0.4 copy.96
  4.6 2.1 %collective-permute-start.5 = (f32[3,32,16,1]{1,2,3,0:T(8,128)S(1)}, f32[3,32,16,1]{1,2,3,0:T(8,128)S(1)}, u32[]{:S(2)}, u32[]{:S(2)}) collective-permute-start(f32[3,32,16,1]{1,2,3,0:T(8,128)S(1)} %copy.96), channel_id=1, source_target_pairs={{4,0},{8,4},{12,8},{0,12},{5,1},{9,5},{13,9},{1,13},{6,2},{10,6},{... | collective-permute-start | bytes 18440 | tf_op jit(solution)/shard_map/ppermute | solution.py:22
  7.4 3.3 %collective-permute-start.1 = (s32[16,1]{1,0:T(8,128)S(1)}, s32[16,1]{1,0:T(8,128)S(1)}, u32[]{:S(2)}, u32[]{:S(2)}) collective-permute-start(s32[16,1]{1,0:T(8,128)S(1)} %get-tuple-element.326), channel_id=1, source_target_pairs={{4,0},{8,4},{12,8},{0,12},{5,1},{9,5},{13,9},{1,13},{6,2},{10,6},{... | collective-permute-start | bytes 200 | tf_op jit(solution)/shard_map/ppermute | solution.py:22
  10.9 2.7 %copy.77 = f32[3,32,16,128]{1,0,3,2:T(4,128)} copy(f32[3,32,16,128]{3,2,1,0:T(8,128)S(1)} %pad_maximum_fusion.1) | data formatting | bytes 1572864 | tf_op jit(solution)/shard_map/concatenate | solution.py:127
  13.6 10.9 %all_gather.10 = f32[3,32,1,512]{3,1,2,0:T(8,128)S(1)} all-gather(f32[3,32,1,128]{3,1,2,0:T(8,128)S(1)} %bitcast.105), channel_id=1, replica_groups=mesh['member'=2,'lon'=4,'lat'=4] {'lon'}, dimensions={3}, use_global_device_ids=true | all-gather | bytes 245760 | tf_op jit(solution)/shard_map/all_gather | solution.py:130
  24.5 9.0 %all_gather.9 = s32[1,512]{1,0:T(1,128)S(1)} all-gather(s32[1,128]{1,0:T(1,128)S(1)} %slice.749), channel_id=1, replica_groups=mesh['member'=2,'lon'=4,'lat'=4] {'lon'}, dimensions={1}, use_global_device_ids=true | all-gather | bytes 2560 | tf_op jit(solution)/shard_map/all_gather | solution.py:124
  33.5 0.4 copy.80
  34.1 6.9 %collective-permute-start.3 = (s32[1,130]{1,0:T(1,128)S(1)}, s32[1,130]{1,0:T(1,128)S(1)}, u32[]{:S(2)}, u32[]{:S(2)}) collective-permute-start(s32[1,130]{1,0:T(1,128)S(1)} %get-tuple-element.324), channel_id=1, source_target_pairs={{1,0},{2,1},{3,2},{0,3},{5,4},{6,5},{7,6},{4,7},{9,8},{10,9},{11,1... | collective-permute-start | bytes 1568 | tf_op jit(solution)/shard_map/ppermute | solution.py:22
  41.0 1.4 %gather_fusion.4 = f32[128,3,32]{2,1,0:T(4,128)} fusion(f32[3,32,512]{1,0,2:T(4,128)S(1)} %bitcast.100, s32[1024]{0:T(1024)S(1)} %pad_clamp_fusion.2), kind=kCustom, calls=%fused_computation.4 | custom fusion | bytes 98816 | tf_op jit(solution)/shard_map/jit(_take)/gather | solution.py:131
  42.4 1.3 gather_fusion.3
  43.7 0.2 collective-permute-start.2
  44.0 0.6 fusion.106
  44.6 0.4 collective-permute-done.2
  44.9 1.4 %add_add_fusion = s32[18,130]{1,0:T(8,128)S(1)} fusion(s32[1,1]{1,0:T(1,128)} %get-tuple-element.328, s32[1,128]{1,0:T(1,128)S(1)} %broadcast_select_fusion.4, s32[1,1]{1,0:T(1,128)} %get-tuple-element.327, s32[16,1]{1,0:T(8,128)S(1)} %collective-permute-done.1, s32[16,128]{1,0:T(8,128)S(1)} %get-tuple-element.199, s32[16,1]{1,0:T(8,128)S(1)} %collective-permute-done, ...), kind=kLoop, calls=%fused_computation.142 | loop fusion | flops 14040 | bytes 18720 | tf_op jit(solution)/shard_map/concatenate | solution.py:35
  46.4 0.2 slice_multiply_fusion.2
  46.7 2.0 %collective-permute-start.10 = (f32[4,12,152]{2,1,0:T(8,128)S(1)}, f32[4,12,152]{2,1,0:T(8,128)S(1)}, u32[]{:S(2)}, u32[]{:S(2)}) collective-permute-start(f32[4,12,152]{2,1,0:T(8,128)S(1)} %get-tuple-element.319), channel_id=1, source_target_pairs={{0,1},{1,2},{2,3},{3,0},{4,5},{5,6},{6,7},{7,4},{8,9},{9,10},{10,1... | collective-permute-start | bytes 87560 | tf_op jit(solution)/shard_map/ppermute | solution.py:20
  48.8 2.8 %pad_maximum_fusion = f32[3,32,16,130]{1,0,3,2:T(4,128)S(1)} fusion(f32[3,32,16,1]{1,0,3,2:T(4,128)S(1)} %copy.78, f32[3,32,16,128]{1,0,3,2:T(4,128)} %copy.77, f32[3,32,16,1]{1,0,3,2:T(4,128)S(1)} %copy.76), kind=kLoop, calls=%fused_computation.65 | loop fusion | flops 399360 | bytes 1597440 | tf_op jit(solution)/shard_map/concatenate | solution.py:18
  51.6 2.0 %copy-done = f32[3,32,16,130]{1,0,3,2:T(4,128)} copy-done((f32[3,32,16,130]{1,0,3,2:T(4,128)}, f32[3,32,16,130]{1,0,3,2:T(4,128)S(1)}, u32[]{:S(2)}) %copy-start) | copy-done | bytes 798744
  53.6 0.9 fusion.97
  54.5 3.9 %copy.85 = f32[3,32,16,130]{3,1,2,0:T(8,128)S(1)} copy(f32[3,32,16,130]{1,0,3,2:T(4,128)} %copy-done) | data formatting | bytes 1597440 | tf_op jit(solution)/shard_map/concatenate | solution.py:18
  58.4 1.7 %collective-permute-start.7 = (f32[3,32,1,130]{1,0,3,2:T(4,128)}, f32[3,32,1,130]{1,0,3,2:T(4,128)}, u32[]{:S(2)}, u32[]{:S(2)}) collective-permute-start(f32[3,32,1,130]{1,0,3,2:T(4,128)} %get-tuple-element.303), channel_id=1, source_target_pairs={{1,0},{2,1},{3,2},{0,3},{5,4},{6,5},{7,6},{4,7},{9,8},{10,9},{11,1... | collective-permute-start | bytes 149768 | tf_op jit(solution)/shard_map/ppermute | solution.py:22
  60.1 0.2 collective-permute-start.6
  60.3 0.1 maximum_select_fusion.3
  60.5 11.0 %all_gather.11 = f32[4,29,512]{2,1,0:T(8,128)S(1)} all-gather(f32[4,29,128]{2,1,0:T(8,128)S(1)} %pad_maximum_fusion.3), channel_id=1, replica_groups=mesh['member'=2,'lon'=4,'lat'=4] {'lon'}, dimensions={2}, use_global_device_ids=true | all-gather | bytes 296960 | tf_op jit(solution)/shard_map/all_gather | solution.py:173
  71.5 54.9 %conditional.1 = (f32[16,128]{1,0:T(8,128)S(1)}, f32[1,16,128]{2,1,0:T(8,128)S(1)}, f32[1,16,128]{2,1,0:T(8,128)S(1)}) conditional(s32[]{:T(128)} %convert_element_type.28, f32[4,40,152]{2,1,0:T(8,128)S(1)} %maximum_select_fusion.3, (f32[4,29,512]{2,1,0:T(8,128)S(1)}, s32[]{:T(128)}) %tuple.33), branch_computations={%region_0.3_spmd, %region_3.7_spmd} | conditional | flops 486406 | bytes 2945535 | solution.py:209
  71.5 3.5 %gather_fusion.2 = f32[512]{0:T(512)S(1)} fusion(f32[512]{0:T(512)S(1)} %bitcast.91, s32[1024]{0:T(1024)S(1)} %pad_clamp_fusion.1), kind=kCustom, calls=%fused_computation.2.clone | custom fusion | bytes 6144 | tf_op jit(solution)/shard_map/cond/branch_1_fun/jit(_take)/gather | solution.py:187
  75.0 3.5 %gather_fusion.1 = f32[512]{0:T(512)S(1)} fusion(f32[512]{0:T(512)S(1)} %bitcast.90, s32[1024]{0:T(1024)S(1)} %pad_clamp_fusion.1), kind=kCustom, calls=%fused_computation.1.clone | custom fusion | bytes 6144 | tf_op jit(solution)/shard_map/cond/branch_1_fun/jit(_take)/gather | solution.py:187
  78.9 47.1 %while.32 = (s32[]{:T(128)}, f32[28,512]{1,0:T(8,128)S(1)}, f32[28,512]{1,0:T(8,128)S(1)}, f32[28,512]{1,0:T(8,128)S(1)}, f32[28,512]{1,0:T(8,128)S(1)}, /*index...) while((s32[]{:T(128)}, f32[28,512]{1,0:T(8,128)S(1)}, ...), condition=%wide.region_5.6_spmd, body=%wide.region_4.5_spmd.sunk | while | flops 307202 | bytes 1282381 | solution.py:110
  79.0 0.1 fusion.111
  79.1 3.5 %gather_fusion = f32[512]{0:T(512)S(1)} fusion(f32[512]{0:T(512)S(1)} %bitcast.89, s32[1024]{0:T(1024)S(1)} %pad_clamp_fusion.4), kind=kCustom, calls=%fused_computation.clone.clone.1 | custom fusion | bytes 6144 | tf_op jit(solution)/shard_map/cond/branch_1_fun/while/body/eval_jaxpr/jit(_take)/gather | solution.py:187
  83.0 3.5 %gather_fusion = f32[512]{0:T(512)S(1)} fusion(f32[512]{0:T(512)S(1)} %bitcast.89, s32[1024]{0:T(1024)S(1)} %pad_clamp_fusion.4), kind=kCustom, calls=%fused_computation.clone.clone.1 | custom fusion | bytes 6144 | tf_op jit(solution)/shard_map/cond/branch_1_fun/while/body/eval_jaxpr/jit(_take)/gather | solution.py:187
  87.0 3.5 %gather_fusion = f32[512]{0:T(512)S(1)} fusion(f32[512]{0:T(512)S(1)} %bitcast.89, s32[1024]{0:T(1024)S(1)} %pad_clamp_fusion.4), kind=kCustom, calls=%fused_computation.clone.clone.1 | custom fusion | bytes 6144 | tf_op jit(solution)/shard_map/cond/branch_1_fun/while/body/eval_jaxpr/jit(_take)/gather | solution.py:187
  90.7 0.1 fusion.111
  90.9 3.5 %gather_fusion = f32[512]{0:T(512)S(1)} fusion(f32[512]{0:T(512)S(1)} %bitcast.89, s32[1024]{0:T(1024)S(1)} %pad_clamp_fusion.4), kind=kCustom, calls=%fused_computation.clone.clone.1 | custom fusion | bytes 6144 | tf_op jit(solution)/shard_map/cond/branch_1_fun/while/body/eval_jaxpr/jit(_take)/gather | solution.py:187
  94.8 3.5 %gather_fusion = f32[512]{0:T(512)S(1)} fusion(f32[512]{0:T(512)S(1)} %bitcast.89, s32[1024]{0:T(1024)S(1)} %pad_clamp_fusion.4), kind=kCustom, calls=%fused_computation.clone.clone.1 | custom fusion | bytes 6144 | tf_op jit(solution)/shard_map/cond/branch_1_fun/while/body/eval_jaxpr/jit(_take)/gather | solution.py:187
  98.7 3.5 %gather_fusion = f32[512]{0:T(512)S(1)} fusion(f32[512]{0:T(512)S(1)} %bitcast.89, s32[1024]{0:T(1024)S(1)} %pad_clamp_fusion.4), kind=kCustom, calls=%fused_computation.clone.clone.1 | custom fusion | bytes 6144 | tf_op jit(solution)/shard_map/cond/branch_1_fun/while/body/eval_jaxpr/jit(_take)/gather | solution.py:187
  102.5 0.1 fusion.111
  102.7 3.5 %gather_fusion = f32[512]{0:T(512)S(1)} fusion(f32[512]{0:T(512)S(1)} %bitcast.89, s32[1024]{0:T(1024)S(1)} %pad_clamp_fusion.4), kind=kCustom, calls=%fused_computation.clone.clone.1 | custom fusion | bytes 6144 | tf_op jit(solution)/shard_map/cond/branch_1_fun/while/body/eval_jaxpr/jit(_take)/gather | solution.py:187
  106.6 3.5 %gather_fusion = f32[512]{0:T(512)S(1)} fusion(f32[512]{0:T(512)S(1)} %bitcast.89, s32[1024]{0:T(1024)S(1)} %pad_clamp_fusion.4), kind=kCustom, calls=%fused_computation.clone.clone.1 | custom fusion | bytes 6144 | tf_op jit(solution)/shard_map/cond/branch_1_fun/while/body/eval_jaxpr/jit(_take)/gather | solution.py:187
  110.5 3.5 %gather_fusion = f32[512]{0:T(512)S(1)} fusion(f32[512]{0:T(512)S(1)} %bitcast.89, s32[1024]{0:T(1024)S(1)} %pad_clamp_fusion.4), kind=kCustom, calls=%fused_computation.clone.clone.1 | custom fusion | bytes 6144 | tf_op jit(solution)/shard_map/cond/branch_1_fun/while/body/eval_jaxpr/jit(_take)/gather | solution.py:187
  114.5 3.5 %gather_fusion = f32[512]{0:T(512)S(1)} fusion(f32[512]{0:T(512)S(1)} %bitcast.89, s32[1024]{0:T(1024)S(1)} %pad_clamp_fusion.4), kind=kCustom, calls=%fused_computation.clone.clone.1 | custom fusion | bytes 6144 | tf_op jit(solution)/shard_map/cond/branch_1_fun/while/body/eval_jaxpr/jit(_take)/gather | solution.py:187
  118.2 0.1 fusion.111
  118.4 3.5 %gather_fusion = f32[512]{0:T(512)S(1)} fusion(f32[512]{0:T(512)S(1)} %bitcast.89, s32[1024]{0:T(1024)S(1)} %pad_clamp_fusion.4), kind=kCustom, calls=%fused_computation.clone.clone.1 | custom fusion | bytes 6144 | tf_op jit(solution)/shard_map/cond/branch_1_fun/while/body/eval_jaxpr/jit(_take)/gather | solution.py:187
  122.3 3.5 %gather_fusion = f32[512]{0:T(512)S(1)} fusion(f32[512]{0:T(512)S(1)} %bitcast.89, s32[1024]{0:T(1024)S(1)} %pad_clamp_fusion.4), kind=kCustom, calls=%fused_computation.clone.clone.1 | custom fusion | bytes 6144 | tf_op jit(solution)/shard_map/cond/branch_1_fun/while/body/eval_jaxpr/jit(_take)/gather | solution.py:187
  126.4 0.6 pad_maximum_fusion.5
  127.0 1.2 slice_select_fusion
  128.3 1.0 broadcast_select_fusion.2
  129.4 0.1 copy.84
  129.5 0.7 fusion.102
  130.4 0.2 maximum_maximum_fusion
  130.6 0.1 slice_bitcast_fusion.13
  130.7 0.1 slice.765
  130.9 0.4 fusion.98
  131.2 0.4 fusion.100
  131.6 0.3 copy-done.7
  131.9 1.6 %fusion.23 = f32[32,16,129]{2,1,0:T(8,128)S(1)} fusion(f32[32,18,130]{2,1,0:T(8,128)S(1)} %fusion.22, f32[32,16,129]{2,0,1:T(8,128)S(1)} %get-tuple-element.331, f32[32,16,129]{2,0,1:T(8,128)S(1)} %get-tuple-element.332, f32[32,16,129]{2,0,1:T(8,128)S(1)} %get-tuple-element.310, f32[32,16,129]{2,0,1:T(8,128)S(1)} %get-tuple-element.309, f32[32]{0:T(128)S(1)} %copy-done.7), kind=kLoop, calls=%fused_computation.82 | loop fusion | flops 594432 | bytes 1849472 | tf_op jit(solution)/shard_map/mul | solution.py:40
  133.5 1.0 fusion.29
  134.5 0.3 fusion.34
  134.8 0.3 fusion.38
  135.1 0.1 constant_dynamic-update-slice_fusion.31
  135.6 0.7 copy-done.10
  (223 shorter events, 5.9 us)
Async XLA Ops:
  0.6 6.6 %copy-start.5 = (s32[16,128]{1,0:T(8,128)S(1)}, s32[16,128]{1,0:T(8,128)}, u32[]{:S(2)}) copy-start(s32[16,128]{1,0:T(8,128)} %param.23) | copy-start | bytes 24580
  0.6 10.0 %copy-start.3 = (f32[2,16,128]{2,1,0:T(8,128)S(1)}, f32[2,16,128]{2,1,0:T(8,128)}, u32[]{:S(2)}) copy-start(f32[2,16,128]{2,1,0:T(8,128)} %param.20) | copy-start | bytes 49156
  0.7 10.0 %copy-start.4 = (f32[16,128]{1,0:T(8,128)S(1)}, f32[16,128]{1,0:T(8,128)}, u32[]{:S(2)}) copy-start(f32[16,128]{1,0:T(8,128)} %param.19) | copy-start | bytes 24580
  0.7 10.1 %copy-start.1 = (f32[2,32,16,128]{3,2,1,0:T(8,128)S(1)}, f32[2,32,16,128]{3,2,1,0:T(8,128)}, u32[]{:S(2)}) copy-start(f32[2,32,16,128]{3,2,1,0:T(8,128)} %param.18) | copy-start | bytes 1572868
  0.7 10.1 %copy-start.2 = (f32[32,16,128]{2,1,0:T(8,128)S(1)}, f32[32,16,128]{2,1,0:T(8,128)}, u32[]{:S(2)}) copy-start(f32[32,16,128]{2,1,0:T(8,128)} %param.17) | copy-start | bytes 786436
  2.8 8.1 %copy-start.9 = (s32[128]{0:T(128)S(1)}, s32[128]{0:T(128)}, u32[]{:S(2)}) copy-start(s32[128]{0:T(128)} %param.25) | copy-start | bytes 1540
  2.8 45.9 %collective-permute-start.4 = (f32[3,32,16,1]{1,2,3,0:T(8,128)S(1)}, f32[3,32,16,1]{1,2,3,0:T(8,128)S(1)}, u32[]{:S(2)}, u32[]{:S(2)}) collective-permute-start(f32[3,32,16,1]{1,2,3,0:T(8,128)S(1)} %copy.95), channel_id=1, source_target_pairs={{0,4},{4,8},{8,12},{12,0},{1,5},{5,9},{9,13},{13,1},{2,6},{6,10},{... | collective-permute-start | bytes 18440 | tf_op jit(solution)/shard_map/ppermute | solution.py:20
  4.6 44.2 %collective-permute-start.5 = (f32[3,32,16,1]{1,2,3,0:T(8,128)S(1)}, f32[3,32,16,1]{1,2,3,0:T(8,128)S(1)}, u32[]{:S(2)}, u32[]{:S(2)}) collective-permute-start(f32[3,32,16,1]{1,2,3,0:T(8,128)S(1)} %copy.96), channel_id=1, source_target_pairs={{4,0},{8,4},{12,8},{0,12},{5,1},{9,5},{13,9},{1,13},{6,2},{10,6},{... | collective-permute-start | bytes 18440 | tf_op jit(solution)/shard_map/ppermute | solution.py:22
  7.4 26.6 %collective-permute-start = (s32[16,1]{1,0:T(8,128)S(1)}, s32[16,1]{1,0:T(8,128)S(1)}, u32[]{:S(2)}, u32[]{:S(2)}) collective-permute-start(s32[16,1]{1,0:T(8,128)S(1)} %get-tuple-element.325), channel_id=1, source_target_pairs={{0,4},{4,8},{8,12},{12,0},{1,5},{5,9},{9,13},{13,1},{2,6},{6,10},{... | collective-permute-start | bytes 200 | tf_op jit(solution)/shard_map/ppermute | solution.py:20
  7.4 26.6 %collective-permute-start.1 = (s32[16,1]{1,0:T(8,128)S(1)}, s32[16,1]{1,0:T(8,128)S(1)}, u32[]{:S(2)}, u32[]{:S(2)}) collective-permute-start(s32[16,1]{1,0:T(8,128)S(1)} %get-tuple-element.326), channel_id=1, source_target_pairs={{4,0},{8,4},{12,8},{0,12},{5,1},{9,5},{13,9},{1,13},{6,2},{10,6},{... | collective-permute-start | bytes 200 | tf_op jit(solution)/shard_map/ppermute | solution.py:22
  10.7 35.8 %collective-permute-start.8 = (f32[4,16,12]{2,1,0:T(8,128)S(1)}, f32[4,16,12]{2,1,0:T(8,128)S(1)}, u32[]{:S(2)}, u32[]{:S(2)}) collective-permute-start(f32[4,16,12]{2,1,0:T(8,128)S(1)} %get-tuple-element.321), channel_id=1, source_target_pairs={{0,4},{4,8},{8,12},{12,0},{1,5},{5,9},{9,13},{13,1},{2,6},{6,10},{... | collective-permute-start | bytes 9224 | tf_op jit(solution)/shard_map/ppermute | solution.py:20
  13.6 32.8 %copy-start.8 = (f32[31]{0:T(128)S(1)}, f32[31]{0:T(128)}, u32[]{:S(2)}) copy-start(f32[31]{0:T(128)} %param.22) | copy-start | bytes 376
  33.9 12.6 %collective-permute-start.9 = (f32[4,16,12]{2,1,0:T(8,128)S(1)}, f32[4,16,12]{2,1,0:T(8,128)S(1)}, u32[]{:S(2)}, u32[]{:S(2)}) collective-permute-start(f32[4,16,12]{2,1,0:T(8,128)S(1)} %get-tuple-element.322), channel_id=1, source_target_pairs={{4,0},{8,4},{12,8},{0,12},{5,1},{9,5},{13,9},{1,13},{6,2},{10,6},{... | collective-permute-start | bytes 9224 | tf_op jit(solution)/shard_map/ppermute | solution.py:22
  34.1 9.6 %collective-permute-start.3 = (s32[1,130]{1,0:T(1,128)S(1)}, s32[1,130]{1,0:T(1,128)S(1)}, u32[]{:S(2)}, u32[]{:S(2)}) collective-permute-start(s32[1,130]{1,0:T(1,128)S(1)} %get-tuple-element.324), channel_id=1, source_target_pairs={{1,0},{2,1},{3,2},{0,3},{5,4},{6,5},{7,6},{4,7},{9,8},{10,9},{11,1... | collective-permute-start | bytes 1568 | tf_op jit(solution)/shard_map/ppermute | solution.py:22
  43.7 1.2 collective-permute-start.2
  46.7 13.6 %collective-permute-start.10 = (f32[4,12,152]{2,1,0:T(8,128)S(1)}, f32[4,12,152]{2,1,0:T(8,128)S(1)}, u32[]{:S(2)}, u32[]{:S(2)}) collective-permute-start(f32[4,12,152]{2,1,0:T(8,128)S(1)} %get-tuple-element.319), channel_id=1, source_target_pairs={{0,1},{1,2},{2,3},{3,0},{4,5},{5,6},{6,7},{7,4},{8,9},{9,10},{10,1... | collective-permute-start | bytes 87560 | tf_op jit(solution)/shard_map/ppermute | solution.py:20
  48.7 11.6 %collective-permute-start.11 = (f32[4,12,152]{2,1,0:T(8,128)S(1)}, f32[4,12,152]{2,1,0:T(8,128)S(1)}, u32[]{:S(2)}, u32[]{:S(2)}) collective-permute-start(f32[4,12,152]{2,1,0:T(8,128)S(1)} %get-tuple-element.320), channel_id=1, source_target_pairs={{1,0},{2,1},{3,2},{0,3},{5,4},{6,5},{7,6},{4,7},{9,8},{10,9},{11,1... | collective-permute-start | bytes 87560 | tf_op jit(solution)/shard_map/ppermute | solution.py:22
  51.6 2.0 %copy-start = (f32[3,32,16,130]{1,0,3,2:T(4,128)}, f32[3,32,16,130]{1,0,3,2:T(4,128)S(1)}, u32[]{:S(2)}) copy-start(f32[3,32,16,130]{1,0,3,2:T(4,128)S(1)} %pad_maximum_fusion) | copy-start | bytes 2396164
  58.4 68.6 %collective-permute-start.7 = (f32[3,32,1,130]{1,0,3,2:T(4,128)}, f32[3,32,1,130]{1,0,3,2:T(4,128)}, u32[]{:S(2)}, u32[]{:S(2)}) collective-permute-start(f32[3,32,1,130]{1,0,3,2:T(4,128)} %get-tuple-element.303), channel_id=1, source_target_pairs={{1,0},{2,1},{3,2},{0,3},{5,4},{6,5},{7,6},{4,7},{9,8},{10,9},{11,1... | collective-permute-start | bytes 149768 | tf_op jit(solution)/shard_map/ppermute | solution.py:22
  60.1 68.3 %collective-permute-start.6 = (f32[3,32,1,130]{1,0,3,2:T(4,128)}, f32[3,32,1,130]{1,0,3,2:T(4,128)}, u32[]{:S(2)}, u32[]{:S(2)}) collective-permute-start(f32[3,32,1,130]{1,0,3,2:T(4,128)} %get-tuple-element.302), channel_id=1, source_target_pairs={{0,1},{1,2},{2,3},{3,0},{4,5},{5,6},{6,7},{7,4},{8,9},{9,10},{10,1... | collective-permute-start | bytes 149768 | tf_op jit(solution)/shard_map/ppermute | solution.py:20
  126.4 4.2 %copy-start.6 = (f32[16,128]{1,0:T(8,128)}, f32[16,128]{1,0:T(8,128)S(1)}, u32[]{:S(2)}) copy-start(f32[16,128]{1,0:T(8,128)S(1)} %get-tuple-element.154) | copy-start | bytes 24580
  131.2 0.7 copy-start.7
  135.6 0.7 copy-start.10
where the time goes:
time: 137 us; the launch traced here: 136 us
  local copies, waits for them, and re-layouts  68.7 us (50%)
  blocking collectives  30.9 us (23%)
  starting transfers between devices  17.8 us (13%)
  other arithmetic  15.7 us (11%)
  between operations  1.95 us (1%)
    gather x14, local copies, waits for them, and re-layouts, strip_path(): jnp.take(edge_row, pair_all, axis=1)  48.9 us
    ppermute x6, starting transfers between devices, with_halo(): lax.ppermute(head, axis, [((i + 1) % count, i) for i in range(count)])  14 us
    all_gather x1, blocking collectives, shards(): lax.all_gather(jnp.concatenate([strip_piece, pair_row], axis=1), 'lon', a...  11 us
    all_gather x1, blocking collectives, shards(): tracer_top = lax.all_gather(top_slab, 'lon', axis=3, tiled=True)  10.9 us
    all_gather x1, blocking collectives, shards(): level_top = lax.all_gather(depth_levels[-1:, :], 'lon', axis=1, tiled=True)  9.01 us
    concatenate x1, local copies, waits for them, and re-layouts, with_halo(): jnp.concatenate([lax.ppermute(tail, axis, [(i, (i + 1) % count) for i in...  3.9 us
    unnamed x39, local copies, waits for them, and re-layouts  3.87 us
    ppermute x6, starting transfers between devices, with_halo(): lax.ppermute(tail, axis, [(i, (i + 1) % count) for i in range(count)])  3.8 us
  transfers between devices with their start and end apart: 12, of which 1 were waited for; matrix products, arithmetic and copies ran while one was open for 53% of the time, Pallas kernels for 0%

commit v1 on v0

v1 whole, which is shorter than its diff:
```python
import functools

import jax
import jax.numpy as jnp
from jax import lax
from jax.experimental import pallas as pl
from jax.experimental.pallas import tpu as pltpu
from jax.sharding import PartitionSpec as P

SUB = 12
LANES = 128
ROWS = 8

fb_step = 0.6
drag_rate = 0.02

E, W, N, S, NE, NW, SE, SW = range(8)


def lane_roll(field, shift):
    return pltpu.roll(field, shift % field.shape[1], 1)


def row_roll(field, shift):
    return pltpu.roll(field, shift % field.shape[0], 0)


def take_lanes(piece, idx):
    return jnp.take_along_axis(piece, idx, axis=1, mode="promise_in_bounds")


def kernel(
    n_lon,
    n_lat,
    tracer,
    velocity,
    surface,
    transport,
    horiz,
    vert,
    levels,
    land,
    fold_pair,
    tracer_new,
    surface_new,
    transport_new,
    nbuf,
    sbuf,
    ewbuf,
    from_n,
    from_s,
    from_e,
    from_w,
    corner,
    fold,
    north_b,
    diff_row,
    inv_pivot,
    primes,
    send_sem,
    recv_sem,
    fold_send,
    fold_recv,
):
    depth_count, tile_rows, tile_cols = tracer.shape
    halves = tile_rows // ROWS
    lon = lax.axis_index("lon")
    lat = lax.axis_index("lat")
    at_top = lat == n_lat - 1
    at_bottom = lat == 0
    east = lax.rem(lon + 1, n_lon)
    west = lax.rem(lon + n_lon - 1, n_lon)
    f32 = jnp.float32
    height_rows = 4 * tile_rows

    def place(lon_to, lat_to):
        return {"lon": lon_to, "lat": lat_to}

    barrier = pltpu.get_barrier_semaphore()

    def greet(lon_to, lat_to):
        pl.semaphore_signal(
            barrier, inc=1, device_id=place(lon_to, lat_to), device_id_type=pl.DeviceIdType.MESH
        )

    greet(east, lat)
    greet(west, lat)

    @pl.when(jnp.logical_not(at_top))
    def _():
        for other in (lon, east, west):
            greet(other, lat + 1)

    @pl.when(jnp.logical_not(at_bottom))
    def _():
        for other in (lon, east, west):
            greet(other, lat - 1)

    @pl.when(at_top)
    def _():
        for r in range(2, n_lon - 1):
            greet(lax.rem(lon + r, n_lon), lat)

    lane = lax.broadcasted_iota(jnp.int32, (ROWS, LANES), 1)
    sub = lax.broadcasted_iota(jnp.int32, (ROWS, LANES), 0)
    lane_t = lax.broadcasted_iota(jnp.int32, (tile_rows, LANES), 1)
    row_t = lax.broadcasted_iota(jnp.int32, (tile_rows, LANES), 0)

    depth = (levels[...] * (1 - land[0, 0])).astype(f32)
    own = [surface[...], transport[0], transport[1], depth]

    for f in range(4):
        sbuf[pl.ds(f * tile_rows, tile_rows), :] = own[f]
    sbuf[pl.ds(height_rows, depth_count), :] = tracer[:, 0, :]
    sbuf[pl.ds(height_rows + depth_count, depth_count), :] = velocity[1, :, 0, :]
    nbuf[pl.ds(height_rows, depth_count), :] = tracer[:, tile_rows - 1, :]
    nbuf[pl.ds(height_rows + depth_count, depth_count), :] = velocity[1, :, tile_rows - 1, :]

    @pl.when(jnp.logical_not(at_top))
    def _():
        for f in range(4):
            nbuf[pl.ds(f * tile_rows, tile_rows), :] = own[f]

    @pl.when(at_top)
    def _():
        for f in range(4):
            for k in range(tile_rows):
                row = tile_rows - 1 - k
                if f == 2:
                    row = row - 1 if row else tile_rows - 1
                value = sbuf[pl.ds(f * tile_rows + row, 1), :]
                if f == 1 or (f == 2 and k < tile_rows - 1):
                    value = -value
                nbuf[pl.ds(f * tile_rows + k, 1), :] = value

    slot = LANES // 4
    pack = jnp.zeros((tile_rows, LANES), f32)
    for f in range(4):
        pack = jnp.where(lane_t // slot == f, lane_roll(own[f], SUB + slot * f), pack)
    ewbuf[pl.ds(0, tile_rows), :] = pack

    pair_lane = lane // 2
    edge_t = jnp.zeros((ROWS, LANES), f32)
    edge_u = jnp.zeros((ROWS, LANES), f32)
    for k in range(depth_count):
        for r in range(halves):
            m = k * halves + r
            pick = pair_lane == m
            edge_t = jnp.where(pick, lane_roll(tracer[k, pl.ds(r * ROWS, ROWS), :], 2 * m + 1), edge_t)
            edge_u = jnp.where(
                pick, lane_roll(velocity[0, k, pl.ds(r * ROWS, ROWS), :], 2 * m + 1), edge_u
            )
    ewbuf[pl.ds(tile_rows, ROWS), :] = edge_t
    ewbuf[pl.ds(tile_rows + ROWS, ROWS), :] = edge_u

    @pl.when(at_bottom)
    def _():
        from_s[...] = jnp.zeros_like(from_s)
        corner[SE - NE] = jnp.zeros((tile_rows, LANES), f32)
        corner[SW - NE] = jnp.zeros((tile_rows, LANES), f32)

    top = (lat + 1) // n_lat
    bottom = (n_lat - lat) // n_lat
    pl.semaphore_wait(barrier, 2 + 3 * (1 - top) + 3 * (1 - bottom) + (n_lon - 3) * top)

    def copy(src, dst, to, came, lon_to, lat_to):
        return pltpu.make_async_remote_copy(
            src_ref=src,
            dst_ref=dst,
            send_sem=send_sem.at[to],
            recv_sem=recv_sem.at[came],
            device_id=place(lon_to, lat_to),
            device_id_type=pl.DeviceIdType.MESH,
        )

    tile_pack = ewbuf.at[pl.ds(0, tile_rows)]
    to_e = copy(ewbuf, from_w, E, W, east, lat)
    to_w = copy(ewbuf, from_e, W, E, west, lat)
    up = lat + 1
    down = lat - 1
    to_n = copy(nbuf, from_s, N, S, lon, up)
    to_ne = copy(tile_pack, corner.at[SW - NE], NE, SW, east, up)
    to_nw = copy(tile_pack, corner.at[SE - NE], NW, SE, west, up)
    to_s = copy(sbuf, from_n, S, N, lon, down)
    to_se = copy(tile_pack, corner.at[NW - NE], SE, NW, east, down)
    to_sw = copy(tile_pack, corner.at[NE - NE], SW, NE, west, down)
    to_fold = [
        pltpu.make_async_remote_copy(
            src_ref=nbuf,
            dst_ref=fold.at[r - 1],
            send_sem=fold_send.at[r - 1],
            recv_sem=fold_recv.at[r - 1],
            device_id=place(lax.rem(lon + r, n_lon), lat),
            device_id_type=pl.DeviceIdType.MESH,
        )
        for r in range(1, n_lon)
    ]

    @pl.when(at_top)
    def _():
        for one in to_fold:
            one.start()

    @pl.when(jnp.logical_not(at_top))
    def _():
        to_n.start()
        to_ne.start()
        to_nw.start()

    @pl.when(jnp.logical_not(at_bottom))
    def _():
        to_s.start()
        to_se.start()
        to_sw.start()

    to_e.start()
    to_w.start()

    prime = None
    for k in range(depth_count):
        diagonal = jnp.ones((tile_rows, LANES), f32)
        if k > 0:
            above = jnp.where(depth > k, vert[k - 1], 0.0)
            diagonal = diagonal + above
        if k < depth_count - 1:
            below = jnp.where(depth > k + 1, vert[k], 0.0)
            diagonal = diagonal + below
        if k > 0:
            diagonal = diagonal + above * prime
        inverse = 1.0 / diagonal
        inv_pivot[k] = inverse
        if k < depth_count - 1:
            prime = -below * inverse
            primes[k] = prime

    to_e.wait_recv()
    to_w.wait_recv()

    @pl.when(jnp.logical_not(at_bottom))
    def _():
        to_n.wait_recv()
        to_ne.wait_recv()
        to_nw.wait_recv()

    w_slot = lane_t % slot < SUB
    in_halo = jnp.logical_or(lane_t < SUB, lane_t >= LANES - SUB)
    deep_halo = jnp.logical_or(lane_t < SUB + 1, lane_t >= LANES - SUB)

    def side_tiles(e_pack, w_pack):
        both = jnp.where(w_slot, w_pack, e_pack)
        return [jnp.where(in_halo, lane_roll(both, -(slot * f + SUB)), 0.0) for f in range(4)]

    @pl.when(jnp.logical_not(at_top))
    def _():
        to_s.wait_recv()
        to_se.wait_recv()
        to_sw.wait_recv()
        for f, tile in enumerate(side_tiles(corner[NE - NE], corner[NW - NE])):
            north_b[pl.ds(f * tile_rows, tile_rows), :] = tile
        diff_row[...] = jnp.zeros_like(diff_row)

    @pl.when(at_top)
    def _():
        pair = jnp.broadcast_to(fold_pair[...], (ROWS, LANES))
        idx = pair % tile_cols
        tile_a = pair // tile_cols
        tile_b = jnp.where(
            lane < LANES // 2,
            jnp.where(tile_a == 0, n_lon - 1, tile_a - 1),
            jnp.where(tile_a == n_lon - 1, 0, tile_a + 1),
        )
        for one in to_fold:
            one.wait_recv()
        sources = [(nbuf, lon)]
        for r in range(1, n_lon):
            sources.append((fold.at[r - 1], lax.rem(lon + n_lon - r, n_lon)))

        def mirrored(start, with_b):
            part_a = jnp.zeros((ROWS, LANES), f32)
            part_b = jnp.zeros((ROWS, LANES), f32)
            for ref, which in sources:
                piece = take_lanes(ref[pl.ds(start, ROWS), :], idx)
                part_a = jnp.where(tile_a == which, piece, part_a)
                if with_b:
                    part_b = jnp.where(tile_b == which, piece, part_b)
            return part_a, part_b

        for f in range(4):
            for r in range(halves):
                start = f * tile_rows + r * ROWS
                part_a, part_b = mirrored(start, True)
                part_b = jnp.where(deep_halo[:ROWS], part_b, 0.0)
                if f == 1:
                    next_a = lane_roll(part_a, -1)
                    next_b = lane_roll(part_b, -1)
                    part_a = jnp.where(lane == LANES - 1, next_b, next_a)
                    part_b = jnp.where(lane == LANES - 1, next_a, next_b)
                if f == 2 and r == halves - 1:
                    across_a = row_roll(part_a, 1)
                    across_b = row_roll(part_b, 1)
                    own_a = sbuf[pl.ds(3 * tile_rows - 1, 1), :]
                    both = jnp.where(w_slot, from_w[pl.ds(0, tile_rows), :], from_e[pl.ds(0, tile_rows), :])
                    own_b = jnp.where(in_halo, lane_roll(both, -(slot * 2 + SUB)), 0.0)
                    own_b = row_roll(own_b, 1)[:ROWS]
                    diff_row[:, :LANES] = jnp.where(sub == 0, -(across_a + own_a), 0.0)
                    diff_row[:, LANES:] = jnp.where(sub == 0, -(across_b + own_b), 0.0)
                from_n[pl.ds(start, ROWS), :] = part_a
                north_b[pl.ds(start, ROWS), :] = part_b
        for q in range(2 * depth_count // ROWS):
            start = height_rows + q * ROWS
            from_n[pl.ds(start, ROWS), :] = mirrored(start, False)[0]

    own_b = side_tiles(from_e[pl.ds(0, tile_rows), :], from_w[pl.ds(0, tile_rows), :])
    south_b = side_tiles(corner[SE - NE], corner[SW - NE])
    full = SUB // ROWS
    rem = SUB % ROWS

    def ring(own_tile, north_tile, south_tile):
        pieces = [own_tile, north_tile[: full * ROWS]]
        if rem:
            pieces.append(
                jnp.where(
                    sub < rem,
                    north_tile[full * ROWS : (full + 1) * ROWS],
                    south_tile[tile_rows - (full + 1) * ROWS : tile_rows - full * ROWS],
                )
            )
        pieces.append(south_tile[tile_rows - full * ROWS :])
        return jnp.concatenate(pieces, axis=0)

    fields = []
    for f in range(4):
        rows = pl.ds(f * tile_rows, tile_rows)
        fields.append(
            jnp.concatenate(
                [
                    ring(own[f], from_n[rows, :], from_s[rows, :]),
                    ring(own_b[f], north_b[rows, :], south_b[f]),
                ],
                axis=1,
            )
        )
    height, zonal, merid, level_real = fields
    sea = jnp.where(level_real > 0, 1.0, 0.0)
    scale = fb_step / (2.0 * depth_count)
    zonal_mask = sea * lane_roll(sea, -1)
    merid_mask = sea * row_roll(sea, -1)
    zonal_fact = (level_real + lane_roll(level_real, -1)) * scale * zonal_mask
    merid_fact = (level_real + row_roll(level_real, -1)) * scale * merid_mask
    zonal_keep = zonal_mask * (1.0 - drag_rate)
    merid_keep = merid_mask * (1.0 - drag_rate)
    diff = diff_row[...]
    diff_keep = row_roll(merid_keep, 1)[tile_rows : tile_rows + ROWS]
    sea_step = sea * fb_step
    for _ in range(SUB):
        south_v = row_roll(merid, 1)
        south_v = jnp.concatenate(
            [
                south_v[:tile_rows],
                south_v[tile_rows : tile_rows + ROWS] + diff,
                south_v[tile_rows + ROWS :],
            ],
            axis=0,
        )
        diff = diff * diff_keep
        divergence = (zonal - lane_roll(zonal, 1)) + (merid - south_v)
        height = height * sea - sea_step * divergence
        zonal = zonal * zonal_keep - zonal_fact * (lane_roll(height, -1) - height)
        merid = merid * merid_keep - merid_fact * (row_roll(height, -1) - height)
    surface_new[...] = height[:tile_rows, :LANES]
    transport_new[0] = zonal[:tile_rows, :LANES]
    transport_new[1] = merid[:tile_rows, :LANES]

    def face(a, b, va, vb, mix):
        return mix * (b - a) - 0.25 * (va + vb) * (a + b)

    odd = lane % 2 == 1

    def swap(e_edge, w_edge):
        return jnp.where(odd, lane_roll(w_edge, 1), lane_roll(e_edge, -1))

    rows_t = pl.ds(tile_rows, ROWS)
    rows_u = pl.ds(tile_rows + ROWS, ROWS)
    far_t = swap(from_e[rows_t, :], from_w[rows_t, :])
    far_u = swap(from_e[rows_u, :], from_w[rows_u, :])
    level_lane = lane // (2 * halves)
    mix_pack = jnp.zeros((ROWS, LANES), f32)
    for k in range(depth_count):
        mix_pack = jnp.where(level_lane == k, horiz[k], mix_pack)
    own_level = jnp.zeros((ROWS, LANES), f32)
    far_level = jnp.zeros((ROWS, LANES), f32)
    half_lane = pair_lane % halves
    for r in range(halves):
        mine = depth[r * ROWS : (r + 1) * ROWS]
        beside = own_b[3][r * ROWS : (r + 1) * ROWS]
        own_level = jnp.where(
            half_lane == r, jnp.where(odd, mine[:, :1], mine[:, LANES - 1 :]), own_level
        )
        far_level = jnp.where(
            half_lane == r, jnp.where(odd, beside[:, LANES - 1 :], beside[:, :1]), far_level
        )
    level_f = level_lane.astype(f32)
    side_wet = jnp.logical_and(level_f < own_level, level_f < far_level)
    side_mix = jnp.where(odd, -mix_pack, mix_pack)
    side_flux = jnp.where(side_wet, face(edge_t, far_t, edge_u, far_u, side_mix), 0.0)

    k_col = lax.broadcasted_iota(jnp.int32, (depth_count, LANES), 0)
    k_real = k_col.astype(f32)
    mix_col = jnp.zeros((depth_count, LANES), f32)
    for k in range(depth_count):
        mix_col = jnp.where(k_col == k, horiz[k], mix_col)
    t_rows = pl.ds(height_rows, depth_count)
    v_rows = pl.ds(height_rows + depth_count, depth_count)
    north_level = from_n[pl.ds(3 * tile_rows, 1), :]
    south_level = from_s[pl.ds(4 * tile_rows - 1, 1), :]
    north_flux = jnp.where(
        jnp.logical_and(k_real < depth[tile_rows - 1 :], k_real < north_level),
        face(nbuf[t_rows, :], from_n[t_rows, :], nbuf[v_rows, :], from_n[v_rows, :], mix_col),
        0.0,
    )
    south_flux = jnp.where(
        jnp.logical_and(k_real < depth[:1], k_real < south_level),
        face(from_s[t_rows, :], sbuf[t_rows, :], from_s[v_rows, :], sbuf[v_rows, :], mix_col),
        0.0,
    )

    east_level = jnp.minimum(depth, lane_roll(depth, -1))
    up_level = jnp.minimum(depth, row_roll(depth, -1))
    sweep = None
    for k in range(depth_count):
        field = tracer[k]
        zonal_vel = velocity[0, k]
        merid_vel = velocity[1, k]
        side = jnp.concatenate(
            [lane_roll(side_flux, -(2 * (k * halves + r) + 1)) for r in range(halves)], axis=0
        )
        flux_e = face(field, lane_roll(field, -1), zonal_vel, lane_roll(zonal_vel, -1), horiz[k])
        flux_e = jnp.where(lane_t == LANES - 1, side, jnp.where(east_level > k, flux_e, 0.0))
        flux_w = jnp.where(lane_t == 0, side, lane_roll(flux_e, 1))
        flux_n = face(field, row_roll(field, -1), merid_vel, row_roll(merid_vel, -1), horiz[k])
        flux_n = jnp.where(
            row_t == tile_rows - 1, north_flux[k : k + 1], jnp.where(up_level > k, flux_n, 0.0)
        )
        flux_s = jnp.where(row_t == 0, south_flux[k : k + 1], row_roll(flux_n, 1))
        stepped = jnp.where(depth > k, field + ((flux_e - flux_w) + (flux_n - flux_s)), 0.0)
        if k > 0:
            above = jnp.where(depth > k, vert[k - 1], 0.0)
            stepped = stepped + above * sweep
        sweep = stepped * inv_pivot[k]
        tracer_new[k] = sweep
    solved = sweep
    for k in range(depth_count - 2, -1, -1):
        solved = tracer_new[k] - primes[k] * solved
        tracer_new[k] = solved

    to_e.wait_send()
    to_w.wait_send()

    @pl.when(jnp.logical_not(at_top))
    def _():
        to_n.wait_send()
        to_ne.wait_send()
        to_nw.wait_send()

    @pl.when(jnp.logical_not(at_bottom))
    def _():
        to_s.wait_send()
        to_se.wait_send()
        to_sw.wait_send()

    @pl.when(at_top)
    def _():
        for one in to_fold:
            one.wait_send()


def shards(
    n_lon,
    n_lat,
    tracer,
    velocity,
    surface,
    transport,
    horiz_mixing,
    vert_mixing,
    levels,
    land_tiles,
    fold_pair,
):
    depth_count, tile_rows, tile_cols = tracer.shape
    vmem = pl.BlockSpec(memory_space=pltpu.VMEM)
    smem = pl.BlockSpec(memory_space=pltpu.SMEM)
    f32 = jnp.float32
    message = 4 * tile_rows + 2 * depth_count
    return pl.pallas_call(
        functools.partial(kernel, n_lon, n_lat),
        out_shape=(
            jax.ShapeDtypeStruct(tracer.shape, f32),
            jax.ShapeDtypeStruct(surface.shape, f32),
            jax.ShapeDtypeStruct(transport.shape, f32),
        ),
        in_specs=[vmem, vmem, vmem, vmem, smem, smem, vmem, smem, vmem],
        out_specs=(vmem, vmem, vmem),
        scratch_shapes=[
            pltpu.VMEM((message, LANES), f32),
            pltpu.VMEM((message, LANES), f32),
            pltpu.VMEM((tile_rows + 2 * ROWS, LANES), f32),
            pltpu.VMEM((message, LANES), f32),
            pltpu.VMEM((message, LANES), f32),
            pltpu.VMEM((tile_rows + 2 * ROWS, LANES), f32),
            pltpu.VMEM((tile_rows + 2 * ROWS, LANES), f32),
            pltpu.VMEM((4, tile_rows, LANES), f32),
            pltpu.VMEM((n_lon - 1, message, LANES), f32),
            pltpu.VMEM((4 * tile_rows, LANES), f32),
            pltpu.VMEM((ROWS, 2 * LANES), f32),
            pltpu.VMEM(tracer.shape, f32),
            pltpu.VMEM(tracer.shape, f32),
            pltpu.SemaphoreType.DMA((8,)),
            pltpu.SemaphoreType.DMA((8,)),
            pltpu.SemaphoreType.DMA((n_lon - 1,)),
            pltpu.SemaphoreType.DMA((n_lon - 1,)),
        ],
        compiler_params=pltpu.CompilerParams(collective_id=0, has_side_effects=True),
    )(
        tracer,
        velocity,
        surface,
        transport,
        horiz_mixing,
        vert_mixing,
        levels,
        land_tiles,
        fold_pair[None],
    )


def solution(mesh):
    return jax.shard_map(
        functools.partial(shards, mesh.shape["lon"], mesh.shape["lat"]),
        mesh=mesh,
        in_specs=(
            P("member", "lat", "lon"),
            P(None, "member", "lat", "lon"),
            P(("member", "lat"), "lon"),
            P("member", "lat", "lon"),
            P("member"),
            P("member"),
            P("lat", "lon"),
            P("lat", "lon"),
            P("lon"),
        ),
        out_specs=(
            P("member", "lat", "lon"),
            P(("member", "lat"), "lon"),
            P("member", "lat", "lon"),
        ),
        check_vma=False,
    )
```

time: 137 us -> 17.6 us (0.13)
  local copies, waits for them, and re-layouts: 68.7 us -> 3.01 us
  blocking collectives: 30.9 us -> 0 us
  starting transfers between devices: 17.8 us -> 0 us
  other arithmetic: 15.7 us -> 0 us
  Pallas kernels: 0 us -> 13 us
    gather x16 -> x0, local copies, waits for them, and re-layouts: 51.6 us -> none  [the longest x14 48.9 us: strip_path(): jnp.take(edge_row, pair_all, axis=1)]
    all_gather x3 -> x0, blocking collectives: 30.9 us -> none  [the longest x1 11 us: shards(): lax.all_gather(jnp.concatenate([strip_piece, pair_row], axis=1), 'lon', a...]
    ppermute x12 -> x0, starting transfers between devices: 17.8 us -> none  [the longest x6 14 us: with_halo(): lax.ppermute(head, axis, [((i + 1) % count, i) for i in range(count)])]
    pallas_call x0 -> x1, Pallas kernels: none -> 13 us  [shards(): pl.pallas_call(functools.partial(kernel, n_lon, n_lat), out_shape=(jax.Sh...]
    concatenate x2 -> x0, local copies, waits for them, and re-layouts: 6.55 us -> none  [the longest x1 3.9 us: with_halo(): jnp.concatenate([lax.ppermute(tail, axis, [(i, (i + 1) % count) for i in...]
    concatenate x8 -> x0, other arithmetic: 6.27 us -> none  [the longest x2 2.9 us: with_halo(): jnp.concatenate([lax.ppermute(tail, axis, [(i, (i + 1) % count) for i in...]
    slice x80 -> x0, local copies, waits for them, and re-layouts: 5.64 us -> none  [the longest x3 1.36 us: fix_rims(): extended[..., -1:, :1]]
    mul x28 -> x0, other arithmetic: 5.3 us -> none  [the longest x2 2.58 us: face_flux(): wet_near * wet_far]
  transfers between devices with their start and end apart: 12 -> 0, of which waited for: 1 -> 0; matrix products, arithmetic and copies ran while one was open for 53% -> 0% of each run, Pallas kernels for 0% -> 0%
where the time goes in v1:
time: 17.6 us; the launch traced here: 17.3 us
  Pallas kernels  13 us (74%)
  local copies, waits for them, and re-layouts  3.01 us (17%)
  between operations  1.3 us (7%)
    pallas_call x1, Pallas kernels, shards(): pl.pallas_call(functools.partial(kernel, n_lon, n_lat), out_shape=(jax.Sh...  13 us
    unnamed x7, local copies, waits for them, and re-layouts  3.01 us

profile of v1, /device:TPU:7, one launch (start us, length us, event | category | flops | bytes accessed | tf_op | source)
XLA Modules:
  0.0 17.3 jit_solution(9336460467996825165)
XLA Ops:
  1.3 13.0 %shard_map.112 = (f32[32,16,128]{2,1,0:T(8,128)}, f32[16,128]{1,0:T(8,128)}, f32[2,16,128]{2,1,0:T(8,128)}) custom-call(f32[32,16,128]{2,1,0:T(8,128)} %tracer.1, f32[2,32,16,128]{3,2,1,0:T(8,128)} %velocity.1, f32[16,128]{1,0:T(8,128)} %surface.1, f32[2,16,128]{2,1,0:T(8,128)} %transport.1, f32[32]{0:T(128)} %horiz.1, f32[31]{0:T(128)} %vert.1, ...), custom_call_target="tpu_custom_call" | custom-call | tf_op jit(solution)/shard_map/pallas_call | solution.py:495
  14.3 0.0 copy-start.1
  14.3 1.7 %copy.16 = f32[32,16,128]{2,1,0:T(8,128)} copy(f32[32,16,128]{2,1,0:T(8,128)} %get-tuple-element.6) | data formatting | bytes 524288
  16.0 0.0 copy-done.1
  16.0 0.0 copy-start
  16.0 0.6 %copy.17 = f32[16,128]{1,0:T(8,128)} copy(f32[16,128]{1,0:T(8,128)S(1)} %copy-done.1) | data formatting | bytes 16384
  16.6 0.1 copy-done
  16.7 0.6 %copy.18 = f32[2,16,128]{2,1,0:T(8,128)} copy(f32[2,16,128]{2,1,0:T(8,128)S(1)} %copy-done) | data formatting | bytes 32768
Async XLA Ops:
  14.3 1.7 %copy-start.1 = (f32[16,128]{1,0:T(8,128)S(1)}, f32[16,128]{1,0:T(8,128)}, u32[]{:S(2)}) copy-start(f32[16,128]{1,0:T(8,128)} %get-tuple-element.7) | copy-start | bytes 24580
  16.0 0.7 %copy-start = (f32[2,16,128]{2,1,0:T(8,128)S(1)}, f32[2,16,128]{2,1,0:T(8,128)}, u32[]{:S(2)}) copy-start(f32[2,16,128]{2,1,0:T(8,128)} %get-tuple-element.8) | copy-start | bytes 49156

commit v2 on v1

--- a/solution.py
+++ b/solution.py
@@ -14,7 +14,7 @@
 fb_step = 0.6
 drag_rate = 0.02
 
-E, W, N, S, NE, NW, SE, SW = range(8)
+E, W, N, S, NE, NW, SE, SW, E2, W2, N2, S2 = range(12)
 
 
 def lane_roll(field, shift):
@@ -32,18 +32,29 @@
 def kernel(
     n_lon,
     n_lat,
+    tracer_in,
+    velocity_in,
+    surface_in,
+    transport_in,
+    horiz_in,
+    vert_in,
+    levels_in,
+    land_in,
+    fold_pair_in,
+    sweeps,
+    primes,
+    surface_new,
+    transport_new,
     tracer,
     velocity,
     surface,
     transport,
+    levels,
+    fold_pair,
     horiz,
     vert,
-    levels,
     land,
-    fold_pair,
-    tracer_new,
-    surface_new,
-    transport_new,
+    inner,
     nbuf,
     sbuf,
     ewbuf,
@@ -56,7 +67,7 @@
     north_b,
     diff_row,
     inv_pivot,
-    primes,
+    in_sem,
     send_sem,
     recv_sem,
     fold_send,
@@ -76,6 +87,21 @@
     def place(lon_to, lat_to):
         return {"lon": lon_to, "lat": lat_to}
 
+    pairs = [
+        (levels_in, levels),
+        (land_in, land),
+        (surface_in, surface),
+        (transport_in, transport),
+        (tracer_in, tracer),
+        (velocity_in, velocity),
+        (fold_pair_in, fold_pair),
+        (horiz_in, horiz),
+        (vert_in, vert),
+    ]
+    loads = [pltpu.make_async_copy(a, b, in_sem.at[i]) for i, (a, b) in enumerate(pairs)]
+    for load in loads:
+        load.start()
+
     barrier = pltpu.get_barrier_semaphore()
 
     def greet(lon_to, lat_to):
@@ -106,15 +132,13 @@
     lane_t = lax.broadcasted_iota(jnp.int32, (tile_rows, LANES), 1)
     row_t = lax.broadcasted_iota(jnp.int32, (tile_rows, LANES), 0)
 
+    for load in loads[:4]:
+        load.wait()
     depth = (levels[...] * (1 - land[0, 0])).astype(f32)
     own = [surface[...], transport[0], transport[1], depth]
 
     for f in range(4):
         sbuf[pl.ds(f * tile_rows, tile_rows), :] = own[f]
-    sbuf[pl.ds(height_rows, depth_count), :] = tracer[:, 0, :]
-    sbuf[pl.ds(height_rows + depth_count, depth_count), :] = velocity[1, :, 0, :]
-    nbuf[pl.ds(height_rows, depth_count), :] = tracer[:, tile_rows - 1, :]
-    nbuf[pl.ds(height_rows + depth_count, depth_count), :] = velocity[1, :, tile_rows - 1, :]
 
     @pl.when(jnp.logical_not(at_top))
     def _():
@@ -138,6 +162,89 @@
     for f in range(4):
         pack = jnp.where(lane_t // slot == f, lane_roll(own[f], SUB + slot * f), pack)
     ewbuf[pl.ds(0, tile_rows), :] = pack
+
+    @pl.when(at_bottom)
+    def _():
+        from_s[...] = jnp.zeros_like(from_s)
+        corner[SE - NE] = jnp.zeros((tile_rows, LANES), f32)
+        corner[SW - NE] = jnp.zeros((tile_rows, LANES), f32)
+
+    top = (lat + 1) // n_lat
+    bottom = (n_lat - lat) // n_lat
+    pl.semaphore_wait(barrier, 2 + 3 * (1 - top) + 3 * (1 - bottom) + (n_lon - 3) * top)
+
+    def copy(src, dst, to, came, lon_to, lat_to):
+        return pltpu.make_async_remote_copy(
+            src_ref=src,
+            dst_ref=dst,
+            send_sem=send_sem.at[to],
+            recv_sem=recv_sem.at[came],
+            device_id=place(lon_to, lat_to),
+            device_id_type=pl.DeviceIdType.MESH,
+        )
+
+    tile_pack = ewbuf.at[pl.ds(0, tile_rows)]
+    edges = pl.ds(tile_rows, 2 * ROWS)
+    first = pl.ds(0, height_rows)
+    later = pl.ds(height_rows, 2 * depth_count)
+    up = lat + 1
+    down = lat - 1
+    to_e = copy(tile_pack, from_w.at[pl.ds(0, tile_rows)], E, W, east, lat)
+    to_w = copy(tile_pack, from_e.at[pl.ds(0, tile_rows)], W, E, west, lat)
+    to_e2 = copy(ewbuf.at[edges], from_w.at[edges], E2, W2, east, lat)
+    to_w2 = copy(ewbuf.at[edges], from_e.at[edges], W2, E2, west, lat)
+    to_n = copy(nbuf.at[first], from_s.at[first], N, S, lon, up)
+    to_n2 = copy(nbuf.at[later], from_s.at[later], N2, S2, lon, up)
+    to_ne = copy(tile_pack, corner.at[SW - NE], NE, SW, east, up)
+    to_nw = copy(tile_pack, corner.at[SE - NE], NW, SE, west, up)
+    to_s = copy(sbuf.at[first], from_n.at[first], S, N, lon, down)
+    to_s2 = copy(sbuf.at[later], from_n.at[later], S2, N2, lon, down)
+    to_se = copy(tile_pack, corner.at[NW - NE], SE, NW, east, down)
+    to_sw = copy(tile_pack, corner.at[NE - NE], SW, NE, west, down)
+
+    def around(part, base):
+        return [
+            pltpu.make_async_remote_copy(
+                src_ref=nbuf.at[part],
+                dst_ref=fold.at[r - 1, part],
+                send_sem=fold_send.at[base + r - 1],
+                recv_sem=fold_recv.at[base + r - 1],
+                device_id=place(lax.rem(lon + r, n_lon), lat),
+                device_id_type=pl.DeviceIdType.MESH,
+            )
+            for r in range(1, n_lon)
+        ]
+
+    to_fold = around(first, 0)
+    to_fold2 = around(later, n_lon - 1)
+
+    @pl.when(at_top)
+    def _():
+        for one in to_fold:
+            one.start()
+
+    @pl.when(jnp.logical_not(at_top))
+    def _():
+        to_n.start()
+        to_ne.start()
+        to_nw.start()
+
+    @pl.when(jnp.logical_not(at_bottom))
+    def _():
+        to_s.start()
+        to_se.start()
+        to_sw.start()
+
+    to_e.start()
+    to_w.start()
+
+    for load in loads[4:]:
+        load.wait()
+    sbuf[pl.ds(height_rows, depth_count), :] = tracer[:, 0, :]
+    sbuf[pl.ds(height_rows + depth_count, depth_count), :] = velocity[1, :, 0, :]
+    nbuf[pl.ds(height_rows, depth_count), :] = tracer[:, tile_rows - 1, :]
+    nbuf[pl.ds(height_rows + depth_count, depth_count), :] = velocity[1, :, tile_rows - 1, :]
+
 
     pair_lane = lane // 2
     edge_t = jnp.zeros((ROWS, LANES), f32)
@@ -153,68 +260,37 @@
     ewbuf[pl.ds(tile_rows, ROWS), :] = edge_t
     ewbuf[pl.ds(tile_rows + ROWS, ROWS), :] = edge_u
 
-    @pl.when(at_bottom)
-    def _():
-        from_s[...] = jnp.zeros_like(from_s)
-        corner[SE - NE] = jnp.zeros((tile_rows, LANES), f32)
-        corner[SW - NE] = jnp.zeros((tile_rows, LANES), f32)
-
-    top = (lat + 1) // n_lat
-    bottom = (n_lat - lat) // n_lat
-    pl.semaphore_wait(barrier, 2 + 3 * (1 - top) + 3 * (1 - bottom) + (n_lon - 3) * top)
-
-    def copy(src, dst, to, came, lon_to, lat_to):
-        return pltpu.make_async_remote_copy(
-            src_ref=src,
-            dst_ref=dst,
-            send_sem=send_sem.at[to],
-            recv_sem=recv_sem.at[came],
-            device_id=place(lon_to, lat_to),
-            device_id_type=pl.DeviceIdType.MESH,
-        )
-
-    tile_pack = ewbuf.at[pl.ds(0, tile_rows)]
-    to_e = copy(ewbuf, from_w, E, W, east, lat)
-    to_w = copy(ewbuf, from_e, W, E, west, lat)
-    up = lat + 1
-    down = lat - 1
-    to_n = copy(nbuf, from_s, N, S, lon, up)
-    to_ne = copy(tile_pack, corner.at[SW - NE], NE, SW, east, up)
-    to_nw = copy(tile_pack, corner.at[SE - NE], NW, SE, west, up)
-    to_s = copy(sbuf, from_n, S, N, lon, down)
-    to_se = copy(tile_pack, corner.at[NW - NE], SE, NW, east, down)
-    to_sw = copy(tile_pack, corner.at[NE - NE], SW, NE, west, down)
-    to_fold = [
-        pltpu.make_async_remote_copy(
-            src_ref=nbuf,
-            dst_ref=fold.at[r - 1],
-            send_sem=fold_send.at[r - 1],
-            recv_sem=fold_recv.at[r - 1],
-            device_id=place(lax.rem(lon + r, n_lon), lat),
-            device_id_type=pl.DeviceIdType.MESH,
-        )
-        for r in range(1, n_lon)
-    ]
 
     @pl.when(at_top)
     def _():
-        for one in to_fold:
+        for one in to_fold2:
             one.start()
 
     @pl.when(jnp.logical_not(at_top))
     def _():
-        to_n.start()
-        to_ne.start()
-        to_nw.start()
+        to_n2.start()
 
     @pl.when(jnp.logical_not(at_bottom))
     def _():
-        to_s.start()
-        to_se.start()
-        to_sw.start()
-
-    to_e.start()
-    to_w.start()
+        to_s2.start()
+
+    to_e2.start()
+    to_w2.start()
+
+    def face(a, b, va, vb, mix):
+        return mix * (b - a) - 0.25 * (va + vb) * (a + b)
+
+    east_level = jnp.where(lane_t == LANES - 1, 0.0, jnp.minimum(depth, lane_roll(depth, -1)))
+    up_level = jnp.where(row_t == tile_rows - 1, 0.0, jnp.minimum(depth, row_roll(depth, -1)))
+    for k in range(depth_count):
+        field = tracer[k]
+        zonal_vel = velocity[0, k]
+        merid_vel = velocity[1, k]
+        flux_e = face(field, lane_roll(field, -1), zonal_vel, lane_roll(zonal_vel, -1), horiz[k])
+        flux_e = jnp.where(east_level > k, flux_e, 0.0)
+        flux_n = face(field, row_roll(field, -1), merid_vel, row_roll(merid_vel, -1), horiz[k])
+        flux_n = jnp.where(up_level > k, flux_n, 0.0)
+        inner[k] = field + ((flux_e - lane_roll(flux_e, 1)) + (flux_n - row_roll(flux_n, 1)))
 
     prime = None
     for k in range(depth_count):
@@ -232,6 +308,7 @@
         if k < depth_count - 1:
             prime = -below * inverse
             primes[k] = prime
+    primes[depth_count - 1] = jnp.zeros((tile_rows, LANES), f32)
 
     to_e.wait_recv()
     to_w.wait_recv()
@@ -259,32 +336,32 @@
             north_b[pl.ds(f * tile_rows, tile_rows), :] = tile
         diff_row[...] = jnp.zeros_like(diff_row)
 
+    sources = [(nbuf, lon)]
+    for r in range(1, n_lon):
+        sources.append((fold.at[r - 1], lax.rem(lon + n_lon - r, n_lon)))
+    pair = jnp.broadcast_to(fold_pair[...], (ROWS, LANES))
+    idx = pair % tile_cols
+    tile_a = pair // tile_cols
+    tile_b = jnp.where(
+        lane < LANES // 2,
+        jnp.where(tile_a == 0, n_lon - 1, tile_a - 1),
+        jnp.where(tile_a == n_lon - 1, 0, tile_a + 1),
+    )
+
+    def mirrored(start, with_b):
+        part_a = jnp.zeros((ROWS, LANES), f32)
+        part_b = jnp.zeros((ROWS, LANES), f32)
+        for ref, which in sources:
+            piece = take_lanes(ref[pl.ds(start, ROWS), :], idx)
+            part_a = jnp.where(tile_a == which, piece, part_a)
+            if with_b:
+                part_b = jnp.where(tile_b == which, piece, part_b)
+        return part_a, part_b
+
     @pl.when(at_top)
     def _():
-        pair = jnp.broadcast_to(fold_pair[...], (ROWS, LANES))
-        idx = pair % tile_cols
-        tile_a = pair // tile_cols
-        tile_b = jnp.where(
-            lane < LANES // 2,
-            jnp.where(tile_a == 0, n_lon - 1, tile_a - 1),
-            jnp.where(tile_a == n_lon - 1, 0, tile_a + 1),
-        )
         for one in to_fold:
             one.wait_recv()
-        sources = [(nbuf, lon)]
-        for r in range(1, n_lon):
-            sources.append((fold.at[r - 1], lax.rem(lon + n_lon - r, n_lon)))
-
-        def mirrored(start, with_b):
-            part_a = jnp.zeros((ROWS, LANES), f32)
-            part_b = jnp.zeros((ROWS, LANES), f32)
-            for ref, which in sources:
-                piece = take_lanes(ref[pl.ds(start, ROWS), :], idx)
-                part_a = jnp.where(tile_a == which, piece, part_a)
-                if with_b:
-                    part_b = jnp.where(tile_b == which, piece, part_b)
-            return part_a, part_b
-
         for f in range(4):
             for r in range(halves):
                 start = f * tile_rows + r * ROWS
@@ -306,10 +383,6 @@
                     diff_row[:, LANES:] = jnp.where(sub == 0, -(across_b + own_b), 0.0)
                 from_n[pl.ds(start, ROWS), :] = part_a
                 north_b[pl.ds(start, ROWS), :] = part_b
-        for q in range(2 * depth_count // ROWS):
-            start = height_rows + q * ROWS
-            from_n[pl.ds(start, ROWS), :] = mirrored(start, False)[0]
-
     own_b = side_tiles(from_e[pl.ds(0, tile_rows), :], from_w[pl.ds(0, tile_rows), :])
     south_b = side_tiles(corner[SE - NE], corner[SW - NE])
     full = SUB // ROWS
@@ -371,8 +444,24 @@
     transport_new[0] = zonal[:tile_rows, :LANES]
     transport_new[1] = merid[:tile_rows, :LANES]
 
-    def face(a, b, va, vb, mix):
-        return mix * (b - a) - 0.25 * (va + vb) * (a + b)
+    to_e2.wait_recv()
+    to_w2.wait_recv()
+
+    @pl.when(jnp.logical_not(at_bottom))
+    def _():
+        to_n2.wait_recv()
+
+    @pl.when(jnp.logical_not(at_top))
+    def _():
+        to_s2.wait_recv()
+
+    @pl.when(at_top)
+    def _():
+        for one in to_fold2:
+            one.wait_recv()
+        for q in range(2 * depth_count // ROWS):
+            start = height_rows + q * ROWS
+            from_n[pl.ds(start, ROWS), :] = mirrored(start, False)[0]
 
     odd = lane % 2 == 1
 
@@ -403,6 +492,7 @@
     side_wet = jnp.logical_and(level_f < own_level, level_f < far_level)
     side_mix = jnp.where(odd, -mix_pack, mix_pack)
     side_flux = jnp.where(side_wet, face(edge_t, far_t, edge_u, far_u, side_mix), 0.0)
+    side_flux = jnp.where(odd, -side_flux, side_flux)
 
     k_col = lax.broadcasted_iota(jnp.int32, (depth_count, LANES), 0)
     k_real = k_col.astype(f32)
@@ -424,54 +514,74 @@
         0.0,
     )
 
-    east_level = jnp.minimum(depth, lane_roll(depth, -1))
-    up_level = jnp.minimum(depth, row_roll(depth, -1))
+    rim = jnp.logical_or(lane_t == 0, lane_t == LANES - 1)
     sweep = None
     for k in range(depth_count):
-        field = tracer[k]
-        zonal_vel = velocity[0, k]
-        merid_vel = velocity[1, k]
         side = jnp.concatenate(
             [lane_roll(side_flux, -(2 * (k * halves + r) + 1)) for r in range(halves)], axis=0
         )
-        flux_e = face(field, lane_roll(field, -1), zonal_vel, lane_roll(zonal_vel, -1), horiz[k])
-        flux_e = jnp.where(lane_t == LANES - 1, side, jnp.where(east_level > k, flux_e, 0.0))
-        flux_w = jnp.where(lane_t == 0, side, lane_roll(flux_e, 1))
-        flux_n = face(field, row_roll(field, -1), merid_vel, row_roll(merid_vel, -1), horiz[k])
-        flux_n = jnp.where(
-            row_t == tile_rows - 1, north_flux[k : k + 1], jnp.where(up_level > k, flux_n, 0.0)
-        )
-        flux_s = jnp.where(row_t == 0, south_flux[k : k + 1], row_roll(flux_n, 1))
-        stepped = jnp.where(depth > k, field + ((flux_e - flux_w) + (flux_n - flux_s)), 0.0)
+        ends = jnp.where(
+            row_t == tile_rows - 1,
+            north_flux[k : k + 1],
+            jnp.where(row_t == 0, -south_flux[k : k + 1], 0.0),
+        )
+        stepped = inner[k] + (jnp.where(rim, side, 0.0) + ends)
+        stepped = jnp.where(depth > k, stepped, 0.0)
         if k > 0:
             above = jnp.where(depth > k, vert[k - 1], 0.0)
             stepped = stepped + above * sweep
         sweep = stepped * inv_pivot[k]
-        tracer_new[k] = sweep
-    solved = sweep
-    for k in range(depth_count - 2, -1, -1):
-        solved = tracer_new[k] - primes[k] * solved
-        tracer_new[k] = solved
+        sweeps[k] = sweep
 
     to_e.wait_send()
     to_w.wait_send()
+    to_e2.wait_send()
+    to_w2.wait_send()
 
     @pl.when(jnp.logical_not(at_top))
     def _():
         to_n.wait_send()
+        to_n2.wait_send()
         to_ne.wait_send()
         to_nw.wait_send()
 
     @pl.when(jnp.logical_not(at_bottom))
     def _():
         to_s.wait_send()
+        to_s2.wait_send()
         to_se.wait_send()
         to_sw.wait_send()
 
     @pl.when(at_top)
     def _():
-        for one in to_fold:
+        for one in to_fold + to_fold2:
             one.wait_send()
+
+
+CHUNK = 8
+
+
+def finish(sweeps, primes, surface, transport, tracer_out, surface_out, transport_out, solution_buf, sem):
+    depth_count = sweeps.shape[0]
+    copies = [
+        pltpu.make_async_copy(surface, surface_out, sem.at[0]),
+        pltpu.make_async_copy(transport, transport_out, sem.at[1]),
+    ]
+    for one in copies:
+        one.start()
+    solved = None
+    for k in range(depth_count - 1, -1, -1):
+        solved = sweeps[k] if solved is None else sweeps[k] - primes[k] * solved
+        solution_buf[k] = solved
+        if k % CHUNK == 0:
+            part = pl.ds(k, min(CHUNK, depth_count - k))
+            one = pltpu.make_async_copy(
+                solution_buf.at[part], tracer_out.at[part], sem.at[2 + k // CHUNK]
+            )
+            one.start()
+            copies.append(one)
+    for one in copies:
+        one.wait()
 
 
 def shards(
@@ -489,19 +599,30 @@
 ):
     depth_count, tile_rows, tile_cols = tracer.shape
     vmem = pl.BlockSpec(memory_space=pltpu.VMEM)
-    smem = pl.BlockSpec(memory_space=pltpu.SMEM)
     f32 = jnp.float32
     message = 4 * tile_rows + 2 * depth_count
-    return pl.pallas_call(
+    held = pl.BlockSpec(memory_space=pltpu.HBM)
+    sweeps, primes, height, flow = pl.pallas_call(
         functools.partial(kernel, n_lon, n_lat),
         out_shape=(
-            jax.ShapeDtypeStruct(tracer.shape, f32),
-            jax.ShapeDtypeStruct(surface.shape, f32),
-            jax.ShapeDtypeStruct(transport.shape, f32),
+            pltpu.VMEM(tracer.shape, f32),
+            pltpu.VMEM(tracer.shape, f32),
+            pltpu.VMEM(surface.shape, f32),
+            pltpu.VMEM(transport.shape, f32),
         ),
-        in_specs=[vmem, vmem, vmem, vmem, smem, smem, vmem, smem, vmem],
-        out_specs=(vmem, vmem, vmem),
+        in_specs=[held] * 9,
+        out_specs=(vmem,) * 4,
         scratch_shapes=[
+            pltpu.VMEM(tracer.shape, f32),
+            pltpu.VMEM(velocity.shape, f32),
+            pltpu.VMEM(surface.shape, f32),
+            pltpu.VMEM(transport.shape, f32),
+            pltpu.VMEM(levels.shape, jnp.int32),
+            pltpu.VMEM((1, tile_cols), jnp.int32),
+            pltpu.SMEM(horiz_mixing.shape, f32),
+            pltpu.SMEM(vert_mixing.shape, f32),
+            pltpu.SMEM((1, 1), jnp.int32),
+            pltpu.VMEM(tracer.shape, f32),
             pltpu.VMEM((message, LANES), f32),
             pltpu.VMEM((message, LANES), f32),
             pltpu.VMEM((tile_rows + 2 * ROWS, LANES), f32),
@@ -514,11 +635,11 @@
             pltpu.VMEM((4 * tile_rows, LANES), f32),
             pltpu.VMEM((ROWS, 2 * LANES), f32),
             pltpu.VMEM(tracer.shape, f32),
-            pltpu.VMEM(tracer.shape, f32),
-            pltpu.SemaphoreType.DMA((8,)),
-            pltpu.SemaphoreType.DMA((8,)),
-            pltpu.SemaphoreType.DMA((n_lon - 1,)),
-            pltpu.SemaphoreType.DMA((n_lon - 1,)),
+            pltpu.SemaphoreType.DMA((9,)),
+            pltpu.SemaphoreType.DMA((12,)),
+            pltpu.SemaphoreType.DMA((12,)),
+            pltpu.SemaphoreType.DMA((2 * (n_lon - 1),)),
+            pltpu.SemaphoreType.DMA((2 * (n_lon - 1),)),
         ],
         compiler_params=pltpu.CompilerParams(collective_id=0, has_side_effects=True),
     )(
@@ -532,6 +653,20 @@
         land_tiles,
         fold_pair[None],
     )
+    return pl.pallas_call(
+        finish,
+        out_shape=(
+            jax.ShapeDtypeStruct(tracer.shape, f32),
+            jax.ShapeDtypeStruct(surface.shape, f32),
+            jax.ShapeDtypeStruct(transport.shape, f32),
+        ),
+        in_specs=[vmem] * 4,
+        out_specs=(held,) * 3,
+        scratch_shapes=[
+            pltpu.VMEM(tracer.shape, f32),
+            pltpu.SemaphoreType.DMA((2 + pl.cdiv(depth_count, CHUNK),)),
+        ],
+    )(*(pltpu.with_memory_space_constraint(x, pltpu.VMEM) for x in (sweeps, primes, height, flow)))
 
 
 def solution(mesh):

time: 17.6 us -> 13.1 us (0.74)
  the two profiles are of different devices: /device:TPU:7 before, /device:TPU:1 now
where the time goes in v2:
time: 13.1 us; the launch traced here: 12.9 us
  Pallas kernels  11.6 us (89%)
  between operations  1.29 us (10%)
    pallas_call x1, Pallas kernels, shards(): pl.pallas_call(functools.partial(kernel, n_lon, n_lat), out_shape=(pltpu....  10.9 us
    pallas_call x1, Pallas kernels, shards(): pl.pallas_call(finish, out_shape=(jax.ShapeDtypeStruct(tracer.shape, f32)...  0.76 us

profile of v2, /device:TPU:1, one launch (start us, length us, event | category | flops | bytes accessed | tf_op | source)
XLA Modules:
  0.0 12.9 jit_solution(10130878511889176760)
XLA Ops:
  1.3 10.9 %shard_map.112 = (f32[32,16,128]{2,1,0:T(8,128)S(1)}, f32[32,16,128]{2,1,0:T(8,128)S(1)}, f32[16,128]{1,0:T(8,128)S(1)}, f32[2,16,128]{2,1,0:T(8,128)S(1)}) custom-call(f32[32,16,128]{2,1,0:T(8,128)} %tracer_in.1, f32[2,32,16,128]{3,2,1,0:T(8,128)} %velocity_in.1, f32[16,128]{1,0:T(8,128)} %surface_in.1, f32[2,16,128]{2,1,0:T(8,128)} %transport_in.1, ...), custom_call_target="tpu_custom_call" | custom-call | tf_op jit(solution)/shard_map/pallas_call | solution.py:605
  12.2 0.8 %shard_map.113 = (f32[32,16,128]{2,1,0:T(8,128)}, f32[16,128]{1,0:T(8,128)}, f32[2,16,128]{2,1,0:T(8,128)}) custom-call(f32[32,16,128]{2,1,0:T(8,128)S(1)} %get-tuple-element.7.sweeps, f32[32,16,128]{2,1,0:T(8,128)S(1)} %get-tuple-element.8.primes, f32[16,128]{1,0:T(8,128)S(1)} %get-tuple-element.9.surface, f32[2,16,128]{2,1,0:T(8,128)S(1)} %get-tuple-element.10.transport), custom_call_target="tpu_custom_call" | custom-call | tf_op jit(solution)/shard_map/pallas_call | solution.py:656
